TPU v7x, 32 devices: a whole 2x2x4 slice. The times are simulated.
32 devices in a mesh: src: 16 (over z, y, core), sub: 2 (over x).
Axes of the slice: x: 2, y: 2, z: 4, core: 2. Of those that a mesh axis runs over, the one named last changes fastest.
Arguments:
- child_rhs: float32 [2, 1024, 4096], P('sub', None, 'src'), may hold values from -6 to 6
- root_rhs: float32 [2048, 4096], P('sub', 'src'), may hold values from -6 to 6
- child_inverse: bfloat16 [2, 1024, 1024], P('sub', 'src'), as said below
- coupling_block: bfloat16 [2, 1024, 1024], P('sub', 'src'), may hold values from -0.1875 to 0.1875
- root_inverse: bfloat16 [2048, 2048], P('sub', 'src'), as said below
- child_orders: int32 [2], P('sub'), may hold values from 716 to 1024, as said below
- coupling_rows: int32 [2, 1024], P('sub'), may hold values from 0 to 2047, as said below
Outputs:
- child_solution: float32 [2, 1024, 4096], P('sub', None, 'src')
- root_solution: float32 [2048, 4096], P('sub', 'src')
Inputs may be any that keep to these rules, and one draw needn't show every extreme that they name: Each child_inverse[j] is lower triangular: zero above the diagonal, diagonal entries between 0.8 and 1.25. `root_inverse`: lower triangular: zero above the diagonal, diagonal entries between 0.8 and 1.25. `coupling_rows`: each row holds 1024 distinct root rows in increasing order. `child_orders`: some child has order 1024.
All inputs are finite; a program needn't handle non-finite values.
Results may differ from a plain program's by a relative error of at most 0.0093.
Values may be sent and summed in bfloat16 or wider, within the bound.
A program may use at most 64 MiB of HBM per device.

v0:
```python
import functools
import jax
import jax.numpy as jnp
from jax import lax
from jax.experimental import pallas as pl
from jax.experimental.pallas import tpu as pltpu
from jax.sharding import PartitionSpec as P

MESH = pl.DeviceIdType.MESH
F32 = jnp.float32
BF16 = jnp.bfloat16


def dot_t(left, right):
    return lax.dot_general(left, right, (((1,), (1,)), ((), ())), preferred_element_type=F32)


def dot_n(left, right):
    return jnp.dot(left, right, preferred_element_type=F32)


def kernel(
    lines, rhs_ref, rrhs_ref, inv_ref, cpl_ref, rinv_ref, order_ref, rows_ref, child_out, root_out,
    inv, cpl, root, hot, src_t, solved_t, upd_t, placed_t, give, take, rr_t, sol_t, sol_b, res_t,
    recv, swap_s, send_z, send_y, send_x, send_c, ex_s, ex_r, bk_s, bk_r, lay,
):
    me, x = lax.axis_index("src"), lax.axis_index("sub")
    core, y, z = me % 2, (me // 2) % 2, me // 4
    strip = inv_ref.shape[0]
    order = inv_ref.shape[1]
    width = rinv_ref.shape[1]
    part = root.shape[1]
    half = order // 2
    cols = rhs_ref.shape[1]
    hcols = cols // 2
    own_rows = rrhs_ref.shape[0]
    blocks = root.shape[0]
    tile = 256
    here = pl.multiple_of(x * hcols, hcols)
    there = pl.multiple_of((1 - x) * hcols, hcols)

    def src_of(zz, yy, cc):
        return (zz * 2 + yy) * 2 + cc

    def dev(zz, yy, cc, xx):
        return {"src": src_of(zz, yy, cc), "sub": xx}

    barrier = pltpu.get_barrier_semaphore()

    def hello(device):
        pl.semaphore_signal(barrier, inc=1, device_id=device, device_id_type=MESH)

    hello(dev(z, 1 - y, core, x))
    hello(dev(z, y, 1 - core, x))
    hello(dev(z, y, core, 1 - x))

    @pl.when(z > 0)
    def _():
        hello(dev(z - 1, y, core, x))

    @pl.when(z < lines - 1)
    def _():
        hello(dev(z + 1, y, core, x))

    inner = jnp.logical_and(z > 0, z < lines - 1)
    pl.when(inner)(lambda: pl.semaphore_wait(barrier, 5))
    pl.when(jnp.logical_not(inner))(lambda: pl.semaphore_wait(barrier, 4))

    kept = 2 * x
    given = 3 - 2 * x
    swapped = 2 * x + 1
    kept_far = 2 - 2 * x
    given_far = 1 + 2 * x

    def strip_ref(which, s):
        r = pl.multiple_of(s * strip, strip)
        return (inv if which == 0 else cpl).at[pl.ds(r, strip), :]

    def block_ref(b, s):
        return root.at[b, :, pl.ds(pl.multiple_of(s * width, width), width)]

    def lives(b, s):
        return s * width < (b + 1) * part

    def views(which, b, s):
        if which == 0:
            ref = strip_ref(0, s)
            r = pl.multiple_of(s * strip, strip)
            narrow = (s + 1) * strip <= half
            return [(narrow, inv.at[pl.ds(r, strip), pl.ds(0, half)]), (jnp.logical_not(narrow), ref)]
        if which == 1:
            return [(None, strip_ref(1, s))]
        return [(lives(b, s), block_ref(b, s))]

    def under(cond, f):
        if cond is None:
            f()
        else:
            pl.when(cond)(f)

    def rsem(which, b, s):
        return recv.at[which if which < 2 else b + 2, s]

    def push(which, b, s, sem, device, wait=False):
        for cond, ref in views(which, b, s):
            def f(ref=ref):
                cp = pltpu.make_async_remote_copy(
                    src_ref=ref, dst_ref=ref, send_sem=sem, recv_sem=rsem(which, b, s),
                    device_id=device, device_id_type=MESH,
                )
                if wait:
                    cp.wait_send()
                else:
                    cp.start()
            under(cond, f)

    def arrive(which, b, s):
        for cond, ref in views(which, b, s):
            def f(ref=ref):
                pltpu.make_async_remote_copy(
                    src_ref=ref, dst_ref=ref, send_sem=recv.at[0, 0], recv_sem=rsem(which, b, s),
                    device_id=dev(z, y, 1 - core, x), device_id_type=MESH,
                ).wait_recv()
            under(cond, f)

    def sends(cls, which, b, zz, far, wait):
        yy = jnp.where(far, 1 - y, y) if not isinstance(far, bool) else (1 - y if far else y)
        s = src_of(zz, yy, core)
        if not far:
            @pl.when(jnp.logical_and(zz <= z, z < lines - 1))
            def _():
                push(which, b, s, send_z.at[cls, 0, zz], dev(z + 1, y, core, x), wait)

            @pl.when(jnp.logical_and(zz >= z, z > 0))
            def _():
                push(which, b, s, send_z.at[cls, 1, zz], dev(z - 1, y, core, x), wait)

            push(which, b, s, send_y.at[cls, zz], dev(z, 1 - y, core, x), wait)
        if which == 2:
            push(which, b, s, send_x.at[cls - 2, int(far), zz], dev(z, y, core, 1 - x), wait)
        push(which, b, s, send_c.at[cls, int(far), zz], dev(z, y, 1 - core, x), wait)

    def own(cls, which, b):
        sends(cls, which, b, z, False, False)

    def relay(cls, which, b, far):
        def step(k, _):
            zz = z + ((k + 1) // 2) * (1 - 2 * (k % 2))

            @pl.when(jnp.logical_and(zz >= 0, zz < lines))
            def _():
                arrive(which, b, src_of(zz, 1 - y if far else y, core))
                sends(cls, which, b, zz, far, False)
            return 0
        lax.fori_loop(0 if far else 1, 2 * lines - 1, step, 0)

    def over_core(which, b):
        def step(k, _):
            arrive(which, b, src_of(k // 2, k % 2, 1 - core))
            return 0
        lax.fori_loop(0, 2 * lines, step, 0)

    def far_plane(cls, b):
        def step(k, _):
            s = src_of(k // 2, k % 2, core)
            arrive(2, b, s)
            push(2, b, s, send_c.at[cls, k % 2, k // 2], dev(z, y, 1 - core, x))
            return 0
        lax.fori_loop(0, 2 * lines, step, 0)

    def swap():
        return pltpu.make_async_remote_copy(
            src_ref=rinv_ref.at[pl.ds(part, part), :], dst_ref=block_ref(swapped, me),
            send_sem=swap_s, recv_sem=recv.at[2 + swapped, me],
            device_id=dev(z, y, core, 1 - x), device_id_type=MESH,
        )

    placing = [
        pltpu.make_async_copy(inv_ref, strip_ref(0, me), lay.at[0]),
        pltpu.make_async_copy(cpl_ref, strip_ref(1, me), lay.at[1]),
        pltpu.make_async_copy(rinv_ref.at[pl.ds(0, part), :], block_ref(kept, me), lay.at[2]),
    ]
    for copy in placing:
        copy.start()
    pl.when(lives(swapped, me))(lambda: swap().start())

    for copy in placing:
        copy.wait()
    own(0, 0, None)
    own(1, 1, None)

    index = rows_ref[...]

    @pl.loop(0, hot.shape[0] // tile)
    def _(i):
        r = pl.multiple_of(i * tile, tile)
        at = lax.broadcasted_iota(jnp.int32, (tile, index.shape[1]), 0) + r
        hot[pl.ds(r, tile), :] = jnp.where(at == index, 1.0, 0.0).astype(BF16)

    alive = lax.broadcasted_iota(jnp.int32, (1, order), 1) < order_ref[0]
    src_t[...] = jnp.where(alive, rhs_ref[...].T, 0.0).astype(BF16)
    own(2, 2, kept)
    relay(0, 0, None, False)
    pl.when(lives(given, me))(lambda: pltpu.make_async_remote_copy(
        src_ref=block_ref(given, me), dst_ref=block_ref(given, me), send_sem=swap_s,
        recv_sem=recv.at[2 + given, me], device_id=dev(z, y, core, 1 - x), device_id_type=MESH,
    ).wait_recv())
    relay(0, 0, None, True)
    relay(1, 1, None, False)
    own(3, 2, given)
    over_core(0, None)
    low = pl.ds(0, half)
    high = pl.ds(half, half)
    solved_t[:, low] = jnp.where(alive[:, :half], dot_t(src_t[:, low], inv[low, low]), 0.0)
    solved_t[:, high] = jnp.where(alive[:, half:], dot_t(src_t[...], inv[high, :]), 0.0)
    relay(1, 1, None, True)
    relay(2, 2, kept, False)
    over_core(1, None)
    upd_t[...] = dot_t(solved_t[...].astype(BF16), cpl[...]).astype(BF16)

    @pl.loop(0, placed_t.shape[1] // tile)
    def _(i):
        r = pl.multiple_of(i * tile, tile)
        placed_t[:, pl.ds(r, tile)] = -dot_t(upd_t[...], hot[pl.ds(r, tile), :])

    mine = pl.ds(pl.multiple_of(x * own_rows, own_rows), own_rows)
    placed_t[:, mine] += rrhs_ref[...].T
    give[...] = placed_t[pl.ds(there, hcols), :].astype(BF16)
    relay(2, 2, kept, True)

    def exchange():
        return pltpu.make_async_remote_copy(
            src_ref=give, dst_ref=take, send_sem=ex_s, recv_sem=ex_r,
            device_id=dev(z, y, core, 1 - x), device_id_type=MESH,
        )

    exchange().start()
    relay(3, 2, given, False)
    relay(3, 2, given, True)
    over_core(2, kept)
    over_core(2, given)
    exchange().wait()
    take[...] = (placed_t[pl.ds(here, hcols), :] + take[...].astype(F32)).astype(BF16)
    far_plane(4, kept_far)
    far_plane(5, given_far)
    over_core(2, kept_far)
    over_core(2, given_far)
    for b in range(blocks):
        upto = pl.ds(0, (b + 1) * part)
        rr_t[:, pl.ds(b * part, part)] = dot_t(take[:, upto], root[b, :, upto]).astype(BF16)

    def back(a):
        piece = sol_b.at[pl.ds(here, hcols), pl.ds(a * part, part)]
        return pltpu.make_async_remote_copy(
            src_ref=piece, dst_ref=piece, send_sem=bk_s.at[a], recv_sem=bk_r.at[a],
            device_id=dev(z, y, core, 1 - x), device_id_type=MESH,
        )

    for a in reversed(range(blocks)):
        at = pl.ds(a * part, part)
        total = dot_n(rr_t[:, at], root[a, :, at])
        for b in range(a + 1, blocks):
            total += dot_n(rr_t[:, pl.ds(b * part, part)], root[b, :, at])
        sol_t[:, at] = total
        sol_b[pl.ds(here, hcols), at] = total.astype(BF16)
        if a + 1 < blocks:
            back(a + 1).start()

    def finish(first):
        rows = pl.ds(first, hcols)
        picked = dot_n(sol_b[rows, :], hot[...]).astype(BF16)
        pulled = dot_n(picked, cpl[...])
        res_t[rows, :] = jnp.where(alive, solved_t[rows, :] - pulled, 0.0).astype(BF16)
        first_half = dot_n(res_t[rows, :], inv[:, low])
        second_half = dot_n(res_t[rows, high], inv[high, high])
        solved_t[rows, low] = jnp.where(alive[:, :half], first_half, 0.0)
        solved_t[rows, high] = jnp.where(alive[:, half:], second_half, 0.0)

    back(0).start()
    finish(here)
    for a in range(blocks):
        back(a).wait_recv()
    finish(there)
    child_out[...] = solved_t[...].T
    src_t[...] = sol_b[:, mine]
    solved_t[...] = src_t[...].astype(F32)
    solved_t[pl.ds(here, hcols), :] = sol_t[:, mine]
    root_out[...] = solved_t[...].T

    pl.when(lives(swapped, me))(lambda: swap().wait_send())
    for a in range(blocks):
        back(a).wait_send()
    for cls, which, b in ((0, 0, None), (1, 1, None), (2, 2, kept), (3, 2, given)):
        for far in (False, True):
            def step(zz, _, cls=cls, which=which, b=b, far=far):
                sends(cls, which, b, zz, far, True)
                return 0
            lax.fori_loop(0, lines, step, 0)
    for cls, b in ((4, kept_far), (5, given_far)):
        def step(k, _, cls=cls, b=b):
            push(2, b, src_of(k // 2, k % 2, core), send_c.at[cls, k % 2, k // 2],
                 dev(z, y, 1 - core, x), True)
            return 0
        lax.fori_loop(0, 2 * lines, step, 0)


def fused(child_rhs, root_rhs, child_inverse, coupling_block, root_inverse, child_orders, coupling_rows):
    n = lax.axis_size("src")
    lines = n // 4
    order = child_inverse.shape[2]
    cols = child_rhs.shape[2]
    own_rows = root_rhs.shape[0]
    root_order = own_rows * lax.axis_size("sub")
    couples = coupling_block.shape[1] * n
    vmem = pl.BlockSpec(memory_space=pltpu.VMEM)
    smem = pl.BlockSpec(memory_space=pltpu.SMEM)
    dma = pltpu.SemaphoreType.DMA
    child_out, root_out = pl.pallas_call(
        functools.partial(kernel, lines),
        out_shape=(
            jax.ShapeDtypeStruct((order, cols), F32),
            jax.ShapeDtypeStruct((own_rows, cols), F32),
        ),
        in_specs=[vmem] * 5 + [smem, vmem],
        out_specs=(vmem, vmem),
        scratch_shapes=[
            pltpu.VMEM((order, order), BF16),
            pltpu.VMEM((couples, order), BF16),
            pltpu.VMEM((4, root_order // 4, root_order), BF16),
            pltpu.VMEM((root_order, couples), BF16),
            pltpu.VMEM((cols, order), BF16),
            pltpu.VMEM((cols, order), F32),
            pltpu.VMEM((cols, couples), BF16),
            pltpu.VMEM((cols, root_order), F32),
            pltpu.VMEM((cols // 2, root_order), BF16),
            pltpu.VMEM((cols // 2, root_order), BF16),
            pltpu.VMEM((cols // 2, root_order), BF16),
            pltpu.VMEM((cols // 2, root_order), F32),
            pltpu.VMEM((cols, root_order), BF16),
            pltpu.VMEM((cols, order), BF16),
            dma((6, n)),
            dma,
            dma((4, 2, lines)),
            dma((4, lines)),
            dma((2, 2, lines)),
            dma((6, 2, lines)),
            dma,
            dma,
            dma((4,)),
            dma((4,)),
            dma((3,)),
        ],
        compiler_params=pltpu.CompilerParams(
            collective_id=0, has_side_effects=True, vmem_limit_bytes=60 * 1024 * 1024
        ),
    )(child_rhs[0], root_rhs, child_inverse[0], coupling_block[0], root_inverse, child_orders, coupling_rows)
    return child_out[None], root_out


def contract_rows(left, right):
    return lax.dot_general(
        left, right, (((0,), (0,)), ((), ())), preferred_element_type=jnp.float32
    )


def on_device(
    child_rhs, root_rhs, child_inverse, coupling_block, root_inverse, child_orders, coupling_rows
):
    inverse = child_inverse[0]
    coupling = coupling_block[0]
    coupling_index = coupling_rows[0]
    columns = child_rhs.shape[2]
    child_order = inverse.shape[1]
    block_rows = root_rhs.shape[0]
    root_order = root_inverse.shape[1] * lax.axis_size("src")
    alive = (lax.iota(jnp.int32, child_order) < child_orders[0])[:, None]
    child_source = jnp.where(alive, child_rhs[0], 0.0).astype(jnp.bfloat16)
    forward = jnp.dot(
        lax.all_gather(inverse, "src", axis=0, tiled=True),
        child_source,
        preferred_element_type=jnp.float32,
    )
    child_solved = jnp.where(alive, forward, 0.0)
    solved_round = child_solved.astype(jnp.bfloat16)
    update = jnp.dot(
        lax.all_gather(coupling, "src", axis=0, tiled=True),
        solved_round,
        preferred_element_type=jnp.float32,
    )
    placed = jnp.zeros((root_order, columns), jnp.float32).at[coupling_index].add(update)
    first_row = lax.axis_index("sub") * block_rows
    own_rows = lax.dynamic_slice_in_dim(placed, first_row, block_rows, 0)
    summand = lax.dynamic_update_slice_in_dim(-placed, root_rhs - own_rows, first_row, 0)
    root_source = lax.psum(summand, "sub").astype(jnp.bfloat16)
    root_forward = jnp.dot(
        lax.all_gather(root_inverse, "src", axis=1, tiled=True),
        root_source,
        preferred_element_type=jnp.float32,
    )
    root_round = root_forward.astype(jnp.bfloat16)
    partial_root = contract_rows(
        lax.all_gather(root_inverse, "src", axis=1, tiled=True), root_round
    )
    root_out = lax.psum_scatter(partial_root, "sub", scatter_dimension=0, tiled=True)
    rounded_all = lax.all_gather(root_out.astype(jnp.bfloat16), "sub", axis=0, tiled=True)
    picked = rounded_all[coupling_index]
    pulled = contract_rows(lax.all_gather(coupling, "src", axis=0, tiled=True), picked)
    residue = jnp.where(alive, child_solved - pulled, 0.0).astype(jnp.bfloat16)
    backward = contract_rows(lax.all_gather(inverse, "src", axis=0, tiled=True), residue)
    child_out = jnp.where(alive, backward, 0.0)[None]
    return (child_out, root_out)


def route(child_rhs, root_rhs, child_inverse, *rest):
    n, subs = lax.axis_size("src"), lax.axis_size("sub")
    order = child_inverse.shape[2]
    fits = subs == 2 and n % 4 == 0 and n >= 8 and root_rhs.shape[0] == order == rest[0].shape[1] * n
    fits = fits and rest[1].shape[1] % 128 == 0 and child_rhs.shape[2] % 256 == 0
    form = fused if fits else on_device
    return form(child_rhs, root_rhs, child_inverse, *rest)


def solution(mesh):
    return jax.shard_map(
        route,
        mesh=mesh,
        in_specs=(
            P("sub", None, "src"),
            P("sub", "src"),
            P("sub", "src", None),
            P("sub", "src", None),
            P("sub", "src"),
            P("sub"),
            P("sub", None),
        ),
        out_specs=(P("sub", None, "src"), P("sub", "src")),
        check_vma=False,
    )
```

profile of v0, /device:TPU:0, one launch (start us, length us, event | category | flops | bytes accessed | tf_op | source)
XLA Modules:
  0.0 101.1 jit_solution(7184992594995879617)
XLA Ops:
  1.3 96.5 %shard_map.86 = (f32[1024,256]{1,0:T(8,128)}, f32[1024,256]{1,0:T(8,128)}) custom-call(f32[1024,256]{1,0:T(8,128)} %bitcast.4, f32[1024,256]{1,0:T(8,128)} %rrhs_ref.1, bf16[64,1024]{1,0:T(8,128)(2,1)} %bitcast.6, bf16[64,1024]{1,0:T(8,128)(2,1)} %bitcast.7, bf16[1024,128]{1,0:T(8,128)(2,1)} %rinv_ref.1, s32[1]{0:T(128)S(6)} %copy.11.order_ref, ...), custom_call_target="tpu_custom_call" | custom-call | tf_op jit(solution)/shard_map/pallas_call | solution.py:318
  97.8 0.0 copy-start
  97.8 2.4 %copy.12 = f32[1,1024,256]{2,1,0:T(8,128)} copy(f32[1,1024,256]{2,1,0:T(8,128)} %bitcast.5) | data formatting | bytes 2097152
  100.2 0.0 copy-done
  100.2 1.0 copy.13
Async XLA Ops:
  97.8 2.4 %copy-start = (f32[1024,256]{1,0:T(8,128)S(1)}, f32[1024,256]{1,0:T(8,128)}, u32[]{:S(2)}) copy-start(f32[1024,256]{1,0:T(8,128)} %get-tuple-element.9) | copy-start | bytes 3145732
where the time goes:
time: 101 us
  Pallas kernels  96.5 us (96%)
  local copies, waits for them, and re-layouts  3.32 us (3%)
  between operations  1.29 us (1%)
    pallas_call x1, Pallas kernels, fused(): pl.pallas_call(functools.partial(kernel, lines), out_shape=(jax.ShapeDtyp...  96.5 us
    unnamed x4, local copies, waits for them, and re-layouts  3.32 us

commit v1 on v0

v1 whole, which is shorter than its diff:
```python
import functools
import jax
import jax.numpy as jnp
from jax import lax
from jax.experimental import pallas as pl
from jax.experimental.pallas import tpu as pltpu
from jax.sharding import PartitionSpec as P

MESH = pl.DeviceIdType.MESH
F32 = jnp.float32
BF16 = jnp.bfloat16

INV, CPL, LAST, B2, B1, B0, CROSS = range(7)


def dot_t(left, right):
    return lax.dot_general(left, right, (((1,), (1,)), ((), ())), preferred_element_type=F32)


def dot_n(left, right):
    return jnp.dot(left, right, preferred_element_type=F32)


def kernel(
    lines, rhs_any, rrhs_any, inv_ref, cpl_ref, rinv_ref, order_ref, rows_ref, child_out, root_out,
    inv, cpl, root, hot, hott, column, rows_peer, rhs_ref, rrhs_ref,
    src_t, solved_t, upd_t, upd_peer, rr_give, rr_take, base_t, take, rr_t, sol_t, sol_b, res_t,
    recv, send_z, send_y, send_x, send_c, early_s, rows_r, rr_r, up_s, up_r, bk_s, bk_r, lay,
):
    me, x = lax.axis_index("src"), lax.axis_index("sub")
    core, y, z = me % 2, (me // 2) % 2, me // 4
    strip = inv_ref.shape[0]
    order = inv_ref.shape[1]
    width = rinv_ref.shape[1]
    part = root.shape[1]
    chunks = root.shape[0]
    per = rinv_ref.shape[0] // part
    block = 2 * part
    cols = rhs_ref.shape[1]
    hcols = cols // 2
    own_rows = rrhs_ref.shape[0]
    here = pl.multiple_of(x * hcols, hcols)
    there = pl.multiple_of((1 - x) * hcols, hcols)

    def src_of(zz, yy, cc):
        return (zz * 2 + yy) * 2 + cc

    def dev(zz, yy, cc, xx):
        return {"src": src_of(zz, yy, cc), "sub": xx}

    loads = [
        pltpu.make_async_copy(rhs_any, rhs_ref, lay.at[0]),
        pltpu.make_async_copy(rrhs_any, rrhs_ref, lay.at[1]),
    ]
    for copy in loads:
        copy.start()

    barrier = pltpu.get_barrier_semaphore()

    def hello(device):
        pl.semaphore_signal(barrier, inc=1, device_id=device, device_id_type=MESH)

    hello(dev(z, 1 - y, core, x))
    hello(dev(z, y, 1 - core, x))
    hello(dev(z, y, core, 1 - x))

    @pl.when(z > 0)
    def _():
        hello(dev(z - 1, y, core, x))

    @pl.when(z < lines - 1)
    def _():
        hello(dev(z + 1, y, core, x))

    def strip_ref(which, s):
        r = pl.multiple_of(s * strip, strip)
        return (inv if which == INV else cpl).at[pl.ds(r, strip), :]

    def cols_of(s):
        return pl.ds(pl.multiple_of(s * width, width), width)

    def chunk_ref(k, s):
        return root.at[k, :, cols_of(s)]

    placing = [
        pltpu.make_async_copy(inv_ref, strip_ref(INV, me), lay.at[2]),
        pltpu.make_async_copy(cpl_ref, strip_ref(CPL, me), lay.at[3]),
    ] + [
        pltpu.make_async_copy(
            rinv_ref.at[pl.ds(i * part, part), :], chunk_ref(per * x + i, me), lay.at[4 + i]
        )
        for i in range(per)
    ]
    for copy in placing:
        copy.start()

    last = chunks - 2 + x
    cross = chunks - 1 - x
    native_of = {B2: x == 1, B1: x == 0, B0: x == 0, LAST: x == 1}
    block_of = {B2: 2, B1: 1, B0: 0}

    def views(which, s):
        if which == INV:
            r = pl.multiple_of(s * strip, strip)
            return [
                (s * strip // part == q, inv.at[pl.ds(r, strip), pl.ds(0, (q + 1) * part)])
                for q in range(order // part)
            ]
        if which == CPL:
            return [(None, strip_ref(CPL, s))]
        if which in (LAST, CROSS):
            k = last if which == LAST else cross
            return [(s * width < (k + 1) * part, chunk_ref(k, s))]
        b = block_of[which]
        full = s * width < b * block + part
        some = jnp.logical_and(s * width >= b * block + part, s * width < (b + 1) * block)
        return [
            (full, root.at[pl.ds(2 * b, 2), :, cols_of(s)]),
            (some, chunk_ref(2 * b + 1, s)),
        ]

    def under(cond, f):
        if cond is None:
            f()
        else:
            pl.when(cond)(f)

    def rsem(which, s):
        if which == LAST:
            return recv.at[LAST + x, s]
        if which == CROSS:
            return recv.at[LAST + 1 - x, s]
        return recv.at[which if which < LAST else which + 1, s]

    def push(which, s, sem, device, wait=False):
        for cond, ref in views(which, s):
            def f(ref=ref):
                cp = pltpu.make_async_remote_copy(
                    src_ref=ref, dst_ref=ref, send_sem=sem, recv_sem=rsem(which, s),
                    device_id=device, device_id_type=MESH,
                )
                if wait:
                    cp.wait_send()
                else:
                    cp.start()
            under(cond, f)

    def arrive(which, s):
        for cond, ref in views(which, s):
            def f(ref=ref):
                pltpu.make_async_remote_copy(
                    src_ref=ref, dst_ref=ref, send_sem=recv.at[0, 0], recv_sem=rsem(which, s),
                    device_id=dev(z, y, 1 - core, x), device_id_type=MESH,
                ).wait_recv()
            under(cond, f)

    other = dev(z, y, core, 1 - x)

    def sends(which, zz, far, wait, mine=False):
        yy = 1 - y if far else y
        s = src_of(zz, yy, core)
        if not far:
            @pl.when(jnp.logical_and(zz <= z, z < lines - 1))
            def _():
                push(which, s, send_z.at[which, 0, zz], dev(z + 1, y, core, x), wait)

            @pl.when(jnp.logical_and(zz >= z, z > 0))
            def _():
                push(which, s, send_z.at[which, 1, zz], dev(z - 1, y, core, x), wait)

            push(which, s, send_y.at[which, zz], dev(z, 1 - y, core, x), wait)
        if which == LAST:
            wanted = jnp.logical_or(zz != z, x == 1) if not far else None
            under(wanted, lambda: push(which, s, send_x.at[int(far), zz], other, wait))
        push(which, s, send_c.at[which, int(far), zz], dev(z, y, 1 - core, x), wait)

    def own(which):
        if which in native_of:
            pl.when(jnp.logical_not(native_of[which]))(lambda: arrive(which, me))
        sends(which, z, False, False)

    def near(which, first=1, stop=None):
        def step(k, _):
            zz = z + ((k + 1) // 2) * (1 - 2 * (k % 2))

            @pl.when(jnp.logical_and(zz >= 0, zz < lines))
            def _():
                arrive(which, src_of(zz, y, core))
                sends(which, zz, False, False)
            return 0
        lax.fori_loop(first, 2 * lines - 1 if stop is None else stop, step, 0)

    def far(which):
        def step(k, _):
            zz = z + ((k + 1) // 2) * (1 - 2 * (k % 2))

            @pl.when(jnp.logical_and(zz >= 0, zz < lines))
            def _():
                arrive(which, src_of(zz, 1 - y, core))
                sends(which, zz, True, False)
            return 0
        lax.fori_loop(0, 2 * lines - 1, step, 0)

    def over_core(which):
        def step(k, _):
            arrive(which, src_of(k // 2, k % 2, 1 - core))
            return 0
        lax.fori_loop(0, 2 * lines, step, 0)

    def crossed():
        def step(k, _):
            s = src_of(k // 2, k % 2, core)

            @pl.when(jnp.logical_or(s != me, x == 0))
            def _():
                arrive(CROSS, s)
                push(CROSS, s, send_c.at[CROSS, k % 2, k // 2], dev(z, y, 1 - core, x))
            return 0
        lax.fori_loop(0, 2 * lines, step, 0)

    def cross_own(wait):
        @pl.when(x == 1)
        def _():
            push(CROSS, me, send_c.at[CROSS, y, z], dev(z, y, 1 - core, x), wait)

    def early(wait):
        def one(which, i):
            push(which, me, early_s.at[i], other, wait)

        @pl.when(x == 1)
        def _():
            one(CROSS, 0)
            one(B2, 1)

        @pl.when(x == 0)
        def _():
            one(B1, 2)
            one(B0, 3)

    def copy_rows():
        return pltpu.make_async_remote_copy(
            src_ref=rows_ref, dst_ref=rows_peer, send_sem=early_s.at[4], recv_sem=rows_r,
            device_id=other, device_id_type=MESH,
        )

    def copy_rrhs():
        return pltpu.make_async_remote_copy(
            src_ref=rr_give, dst_ref=rr_take, send_sem=early_s.at[5], recv_sem=rr_r,
            device_id=other, device_id_type=MESH,
        )

    def copy_update():
        return pltpu.make_async_remote_copy(
            src_ref=upd_t.at[pl.ds(there, hcols), :], dst_ref=upd_peer, send_sem=up_s,
            recv_sem=up_r, device_id=other, device_id_type=MESH,
        )

    def back(a):
        piece = sol_b.at[pl.ds(here, hcols), pl.ds(a * block, block)]
        return pltpu.make_async_remote_copy(
            src_ref=piece, dst_ref=piece, send_sem=bk_s.at[a], recv_sem=bk_r.at[a],
            device_id=other, device_id_type=MESH,
        )

    def turn(slot, index):
        column[slot] = jnp.broadcast_to(index, (width, order)).T

    def scatter_ones(slot):
        @pl.loop(0, order // width)
        def _(i):
            r = pl.multiple_of(i * width, width)
            at = column[slot, pl.ds(r, width), :]
            lane = lax.broadcasted_iota(jnp.int32, (width, width), 1)
            for t in range(hott.shape[2] // width):
                hott[slot, pl.ds(r, width), pl.ds(t * width, width)] = jnp.where(
                    at == lane + t * width, 1.0, 0.0
                ).astype(BF16)

    def gather_ones(index):
        @pl.loop(0, hot.shape[0] // part)
        def _(i):
            r = pl.multiple_of(i * part, part)
            at = lax.broadcasted_iota(jnp.int32, (part, order), 0) + r
            hot[pl.ds(r, part), :] = jnp.where(at == index, 1.0, 0.0).astype(BF16)

    inner = jnp.logical_and(z > 0, z < lines - 1)
    pl.when(inner)(lambda: pl.semaphore_wait(barrier, 5))
    pl.when(jnp.logical_not(inner))(lambda: pl.semaphore_wait(barrier, 4))
    for copy in placing:
        copy.wait()

    own(INV)
    early(False)
    copy_rows().start()
    pl.when(x == 1)(lambda: own(LAST))
    own(CPL)
    cross_own(False)
    for copy in loads:
        copy.wait()
    rr_give[...] = rrhs_ref[:, pl.ds(there, hcols)].T.astype(BF16)
    copy_rrhs().start()
    pl.when(x == 0)(lambda: own(LAST))
    near(INV)
    near(LAST)
    alive = lax.broadcasted_iota(jnp.int32, (1, order), 1) < order_ref[0]
    src_t[...] = jnp.where(alive, rhs_ref[...].T, 0.0).astype(BF16)
    near(CPL)
    far(INV)
    index = rows_ref[...]
    turn(0, index)
    scatter_ones(0)
    own(B2)
    far(LAST)
    near(B2)
    over_core(INV)
    for q in range(order // part):
        at = pl.ds(q * part, part)
        upto = pl.ds(0, (q + 1) * part)
        solved_t[:, at] = jnp.where(
            alive[:, q * part:(q + 1) * part], dot_t(src_t[:, upto], inv[at, upto]), 0.0
        )
    own(B1)
    own(B0)
    far(CPL)
    near(B1)
    near(B0)
    over_core(CPL)
    upd_t[...] = dot_t(solved_t[...].astype(BF16), cpl[...]).astype(BF16)
    copy_update().start()
    far(B2)
    crossed()
    mine = pl.ds(pl.multiple_of(x * own_rows, own_rows), own_rows)
    theirs = pl.ds(pl.multiple_of((1 - x) * own_rows, own_rows), own_rows)
    copy_rrhs().wait_recv()
    base_t[:, mine] = rrhs_ref[:, pl.ds(here, hcols)].T
    base_t[:, theirs] = rr_take[...].astype(F32)
    mine_upd = upd_t[pl.ds(here, hcols), :]
    for i in range(hott.shape[2] // block):
        at = pl.ds(i * block, block)
        base_t[:, at] = base_t[:, at] - dot_n(mine_upd, hott[0, :, at])
    copy_rows().wait_recv()
    turn(1, rows_peer[...])
    scatter_ones(1)
    far(B1)
    far(B0)
    gather_ones(index)
    over_core(LAST)
    over_core(CROSS)
    copy_update().wait_recv()
    for i in range(hott.shape[2] // block):
        at = pl.ds(i * block, block)
        take[:, at] = (base_t[:, at] - dot_n(upd_peer[...], hott[1, :, at])).astype(BF16)

    blocks = chunks // 2
    for b in reversed(range(blocks)):
        if b < blocks - 1:
            over_core((B0, B1, B2)[b])
        for k in (2 * b + 1, 2 * b):
            upto = pl.ds(0, (k + 1) * part)
            rr_t[:, pl.ds(k * part, part)] = dot_t(take[:, upto], root[k, :, upto]).astype(BF16)
        low, high = 2 * b, 2 * b + 1
        r_low, r_high = rr_t[:, pl.ds(low * part, part)], rr_t[:, pl.ds(high * part, part)]
        at_low, at_high = pl.ds(low * part, part), pl.ds(high * part, part)
        s_low = dot_n(r_low, root[low, :, at_low]) + dot_n(r_high, root[high, :, at_low])
        s_high = dot_n(r_high, root[high, :, at_high])
        if b < blocks - 1:
            s_low += sol_t[:, at_low]
            s_high += sol_t[:, at_high]
        sol_t[:, at_low] = s_low
        sol_t[:, at_high] = s_high
        sol_b[pl.ds(here, hcols), at_low] = s_low.astype(BF16)
        sol_b[pl.ds(here, hcols), at_high] = s_high.astype(BF16)
        if b < blocks - 1:
            back(b + 1).start()
        for a in reversed(range(b)):
            at = pl.ds(a * block, block)
            more = dot_n(r_low, root[low, :, at]) + dot_n(r_high, root[high, :, at])
            sol_t[:, at] = more if b == blocks - 1 else sol_t[:, at] + more
    back(0).start()

    def finish(first, picked):
        rows = pl.ds(first, hcols)
        pulled = dot_n(picked.astype(BF16), cpl[...])
        res_t[...] = jnp.where(alive, solved_t[rows, :] - pulled, 0.0).astype(BF16)
        for q in range(order // part):
            at, rest = pl.ds(q * part, part), pl.ds(q * part, order - q * part)
            solved = jnp.where(
                alive[:, q * part:(q + 1) * part], dot_n(res_t[:, rest], inv[rest, at]), 0.0
            )
            child_out[at, rows] = solved.T

    finish(here, dot_n(sol_b[pl.ds(here, hcols), :], hot[...]))
    root_out[:, pl.ds(here, hcols)] = sol_t[:, mine].T
    for a in range(1, blocks):
        back(a).wait_recv()
    upper = pl.ds(block, (blocks - 1) * block)
    picked = dot_n(sol_b[pl.ds(there, hcols), upper], hot[upper, :])
    back(0).wait_recv()
    lower = pl.ds(0, block)
    picked += dot_n(sol_b[pl.ds(there, hcols), lower], hot[lower, :])
    finish(there, picked)
    root_out[:, pl.ds(there, hcols)] = sol_b[pl.ds(there, hcols), mine].astype(F32).T

    early(True)
    cross_own(True)
    copy_rows().wait_send()
    copy_rrhs().wait_send()
    copy_update().wait_send()
    for a in range(blocks):
        back(a).wait_send()
    for which in (INV, CPL, LAST, B2, B1, B0):
        for away in (False, True):
            def step(zz, _, which=which, away=away):
                sends(which, zz, away, True)
                return 0
            lax.fori_loop(0, lines, step, 0)

    def step(k, _):
        s = src_of(k // 2, k % 2, core)

        @pl.when(jnp.logical_or(s != me, x == 0))
        def _():
            push(CROSS, s, send_c.at[CROSS, k % 2, k // 2], dev(z, y, 1 - core, x), True)
        return 0
    lax.fori_loop(0, 2 * lines, step, 0)


def fused(child_rhs, root_rhs, child_inverse, coupling_block, root_inverse, child_orders, coupling_rows):
    n = lax.axis_size("src")
    lines = n // 4
    order = child_inverse.shape[2]
    cols = child_rhs.shape[2]
    own_rows = root_rhs.shape[0]
    root_order = own_rows * lax.axis_size("sub")
    couples = coupling_block.shape[1] * n
    part = root_order // 8
    width = root_inverse.shape[1]
    half = cols // 2
    vmem = pl.BlockSpec(memory_space=pltpu.VMEM)
    smem = pl.BlockSpec(memory_space=pltpu.SMEM)
    anywhere = pl.BlockSpec(memory_space=pl.ANY)
    dma = pltpu.SemaphoreType.DMA
    child_out, root_out = pl.pallas_call(
        functools.partial(kernel, lines),
        out_shape=(
            jax.ShapeDtypeStruct((order, cols), F32),
            jax.ShapeDtypeStruct((own_rows, cols), F32),
        ),
        in_specs=[anywhere] * 2 + [vmem] * 3 + [smem, vmem],
        out_specs=(vmem, vmem),
        scratch_shapes=[
            pltpu.VMEM((order, order), BF16),
            pltpu.VMEM((couples, order), BF16),
            pltpu.VMEM((8, part, root_order), BF16),
            pltpu.VMEM((root_order, couples), BF16),
            pltpu.VMEM((2, couples, root_order), BF16),
            pltpu.VMEM((2, couples, width), jnp.int32),
            pltpu.VMEM((1, couples), jnp.int32),
            pltpu.VMEM((order, cols), F32),
            pltpu.VMEM((own_rows, cols), F32),
            pltpu.VMEM((cols, order), BF16),
            pltpu.VMEM((cols, order), F32),
            pltpu.VMEM((cols, couples), BF16),
            pltpu.VMEM((half, couples), BF16),
            pltpu.VMEM((half, own_rows), BF16),
            pltpu.VMEM((half, own_rows), BF16),
            pltpu.VMEM((half, root_order), F32),
            pltpu.VMEM((half, root_order), BF16),
            pltpu.VMEM((half, root_order), BF16),
            pltpu.VMEM((half, root_order), F32),
            pltpu.VMEM((cols, root_order), BF16),
            pltpu.VMEM((half, order), BF16),
            dma((7, n)),
            dma((6, 2, lines)),
            dma((6, lines)),
            dma((2, lines)),
            dma((7, 2, lines)),
            dma((6,)),
            dma,
            dma,
            dma,
            dma,
            dma((4,)),
            dma((4,)),
            dma((8,)),
        ],
        compiler_params=pltpu.CompilerParams(
            collective_id=0, has_side_effects=True, vmem_limit_bytes=60 * 1024 * 1024
        ),
    )(child_rhs[0], root_rhs, child_inverse[0], coupling_block[0], root_inverse, child_orders, coupling_rows)
    return child_out[None], root_out


def contract_rows(left, right):
    return lax.dot_general(
        left, right, (((0,), (0,)), ((), ())), preferred_element_type=jnp.float32
    )


def on_device(
    child_rhs, root_rhs, child_inverse, coupling_block, root_inverse, child_orders, coupling_rows
):
    inverse = child_inverse[0]
    coupling = coupling_block[0]
    coupling_index = coupling_rows[0]
    columns = child_rhs.shape[2]
    child_order = inverse.shape[1]
    block_rows = root_rhs.shape[0]
    root_order = root_inverse.shape[1] * lax.axis_size("src")
    alive = (lax.iota(jnp.int32, child_order) < child_orders[0])[:, None]
    child_source = jnp.where(alive, child_rhs[0], 0.0).astype(jnp.bfloat16)
    forward = jnp.dot(
        lax.all_gather(inverse, "src", axis=0, tiled=True),
        child_source,
        preferred_element_type=jnp.float32,
    )
    child_solved = jnp.where(alive, forward, 0.0)
    solved_round = child_solved.astype(jnp.bfloat16)
    update = jnp.dot(
        lax.all_gather(coupling, "src", axis=0, tiled=True),
        solved_round,
        preferred_element_type=jnp.float32,
    )
    placed = jnp.zeros((root_order, columns), jnp.float32).at[coupling_index].add(update)
    first_row = lax.axis_index("sub") * block_rows
    own_rows = lax.dynamic_slice_in_dim(placed, first_row, block_rows, 0)
    summand = lax.dynamic_update_slice_in_dim(-placed, root_rhs - own_rows, first_row, 0)
    root_source = lax.psum(summand, "sub").astype(jnp.bfloat16)
    root_forward = jnp.dot(
        lax.all_gather(root_inverse, "src", axis=1, tiled=True),
        root_source,
        preferred_element_type=jnp.float32,
    )
    root_round = root_forward.astype(jnp.bfloat16)
    partial_root = contract_rows(
        lax.all_gather(root_inverse, "src", axis=1, tiled=True), root_round
    )
    root_out = lax.psum_scatter(partial_root, "sub", scatter_dimension=0, tiled=True)
    rounded_all = lax.all_gather(root_out.astype(jnp.bfloat16), "sub", axis=0, tiled=True)
    picked = rounded_all[coupling_index]
    pulled = contract_rows(lax.all_gather(coupling, "src", axis=0, tiled=True), picked)
    residue = jnp.where(alive, child_solved - pulled, 0.0).astype(jnp.bfloat16)
    backward = contract_rows(lax.all_gather(inverse, "src", axis=0, tiled=True), residue)
    child_out = jnp.where(alive, backward, 0.0)[None]
    return (child_out, root_out)


def route(child_rhs, root_rhs, child_inverse, *rest):
    n, subs = lax.axis_size("src"), lax.axis_size("sub")
    order = child_inverse.shape[2]
    fits = subs == 2 and n % 4 == 0 and n >= 8 and root_rhs.shape[0] == order == rest[0].shape[1] * n
    width, part = rest[1].shape[1], order // 4
    fits = fits and width == 128 and part % width == 0 and part * n % order == 0
    fits = fits and child_rhs.shape[2] == 2 * width
    form = fused if fits else on_device
    return form(child_rhs, root_rhs, child_inverse, *rest)


def solution(mesh):
    return jax.shard_map(
        route,
        mesh=mesh,
        in_specs=(
            P("sub", None, "src"),
            P("sub", "src"),
            P("sub", "src", None),
            P("sub", "src", None),
            P("sub", "src"),
            P("sub"),
            P("sub", None),
        ),
        out_specs=(P("sub", None, "src"), P("sub", "src")),
        check_vma=False,
    )
```

time: 101 us -> 79.9 us (0.79)
  the two profiles are of different devices: /device:TPU:0 before, /device:TPU:24 now
where the time goes in v1:
time: 79.9 us; the launch traced here: 79.7 us
  Pallas kernels  75.1 us (94%)
  local copies, waits for them, and re-layouts  3.32 us (4%)
  between operations  1.29 us (2%)
    pallas_call x1, Pallas kernels, fused(): pl.pallas_call(functools.partial(kernel, lines), out_shape=(jax.ShapeDtyp...  75.1 us
    unnamed x4, local copies, waits for them, and re-layouts  3.32 us

profile of v1, /device:TPU:24, one launch (start us, length us, event | category | flops | bytes accessed | tf_op | source)
XLA Modules:
  0.0 79.7 jit_solution(5954146219767105233)
XLA Ops:
  1.3 75.1 %shard_map.86 = (f32[1024,256]{1,0:T(8,128)}, f32[1024,256]{1,0:T(8,128)}) custom-call(f32[1024,256]{1,0:T(8,128)} %bitcast.4, f32[1024,256]{1,0:T(8,128)} %rrhs_any.1, bf16[64,1024]{1,0:T(8,128)(2,1)} %bitcast.6, bf16[64,1024]{1,0:T(8,128)(2,1)} %bitcast.7, bf16[1024,128]{1,0:T(8,128)(2,1)} %rinv_ref.1, s32[1]{0:T(128)S(6)} %copy.11.order_ref, ...), custom_call_target="tpu_custom_call" | custom-call | tf_op jit(solution)/shard_map/pallas_call | solution.py:443
  76.4 0.0 copy-start
  76.4 2.4 %copy.12 = f32[1,1024,256]{2,1,0:T(8,128)} copy(f32[1,1024,256]{2,1,0:T(8,128)} %bitcast.5) | data formatting | bytes 2097152
  78.7 0.0 copy-done
  78.7 1.0 %copy.13 = f32[1024,256]{1,0:T(8,128)} copy(f32[1024,256]{1,0:T(8,128)S(1)} %copy-done) | data formatting | bytes 2097152
Async XLA Ops:
  76.4 2.4 %copy-start = (f32[1024,256]{1,0:T(8,128)S(1)}, f32[1024,256]{1,0:T(8,128)}, u32[]{:S(2)}) copy-start(f32[1024,256]{1,0:T(8,128)} %get-tuple-element.9) | copy-start | bytes 3145732

commit v2 on v1

--- a/solution.py
+++ b/solution.py
@@ -64,13 +64,10 @@
     hello(dev(z, y, 1 - core, x))
     hello(dev(z, y, core, 1 - x))
 
-    @pl.when(z > 0)
-    def _():
-        hello(dev(z - 1, y, core, x))
-
-    @pl.when(z < lines - 1)
-    def _():
-        hello(dev(z + 1, y, core, x))
+    def greet(zz, _):
+        pl.when(zz != z)(lambda: hello(dev(zz, y, core, x)))
+        return 0
+    lax.fori_loop(0, lines, greet, 0)
 
     def strip_ref(which, s):
         r = pl.multiple_of(s * strip, strip)
@@ -156,19 +153,22 @@
 
     other = dev(z, y, core, 1 - x)
 
-    def sends(which, zz, far, wait, mine=False):
+    def sends(which, zz, far, wait):
         yy = 1 - y if far else y
         s = src_of(zz, yy, core)
-        if not far:
+        if not far or which == LAST:
             @pl.when(jnp.logical_and(zz <= z, z < lines - 1))
             def _():
-                push(which, s, send_z.at[which, 0, zz], dev(z + 1, y, core, x), wait)
+                push(which, s, send_z.at[which, int(far), 0, zz], dev(z + 1, y, core, x), wait)
 
             @pl.when(jnp.logical_and(zz >= z, z > 0))
             def _():
-                push(which, s, send_z.at[which, 1, zz], dev(z - 1, y, core, x), wait)
-
-            push(which, s, send_y.at[which, zz], dev(z, 1 - y, core, x), wait)
+                push(which, s, send_z.at[which, int(far), 1, zz], dev(z - 1, y, core, x), wait)
+        if not far:
+            under(
+                zz == z if which == LAST else None,
+                lambda: push(which, s, send_y.at[which, zz], dev(z, 1 - y, core, x), wait),
+            )
         if which == LAST:
             wanted = jnp.logical_or(zz != z, x == 1) if not far else None
             under(wanted, lambda: push(which, s, send_x.at[int(far), zz], other, wait))
@@ -179,27 +179,27 @@
             pl.when(jnp.logical_not(native_of[which]))(lambda: arrive(which, me))
         sends(which, z, False, False)
 
-    def near(which, first=1, stop=None):
+    def either(d, f):
         def step(k, _):
-            zz = z + ((k + 1) // 2) * (1 - 2 * (k % 2))
-
-            @pl.when(jnp.logical_and(zz >= 0, zz < lines))
-            def _():
-                arrive(which, src_of(zz, y, core))
-                sends(which, zz, False, False)
+            zz = z + d * (2 * k - 1)
+            pl.when(jnp.logical_and(zz >= 0, zz < lines))(lambda: f(zz))
             return 0
-        lax.fori_loop(first, 2 * lines - 1 if stop is None else stop, step, 0)
-
-    def far(which):
-        def step(k, _):
-            zz = z + ((k + 1) // 2) * (1 - 2 * (k % 2))
-
-            @pl.when(jnp.logical_and(zz >= 0, zz < lines))
-            def _():
-                arrive(which, src_of(zz, 1 - y, core))
-                sends(which, zz, True, False)
-            return 0
-        lax.fori_loop(0, 2 * lines - 1, step, 0)
+        lax.fori_loop(0, 2, step, 0)
+
+    def near(which, *distances):
+        def one(zz):
+            for away in (False, True) if which == LAST else (False,):
+                arrive(which, src_of(zz, 1 - y if away else y, core))
+                sends(which, zz, away, False)
+        for d in distances:
+            either(d, one)
+
+    def far(which, *distances):
+        def one(zz):
+            arrive(which, src_of(zz, 1 - y, core))
+            sends(which, zz, True, False)
+        for d in distances:
+            one(z) if d == 0 else either(d, one)
 
     def over_core(which):
         def step(k, _):
@@ -283,52 +283,64 @@
             at = lax.broadcasted_iota(jnp.int32, (part, order), 0) + r
             hot[pl.ds(r, part), :] = jnp.where(at == index, 1.0, 0.0).astype(BF16)
 
-    inner = jnp.logical_and(z > 0, z < lines - 1)
-    pl.when(inner)(lambda: pl.semaphore_wait(barrier, 5))
-    pl.when(jnp.logical_not(inner))(lambda: pl.semaphore_wait(barrier, 4))
+    pl.semaphore_wait(barrier, lines + 2)
     for copy in placing:
         copy.wait()
 
     own(INV)
     early(False)
     copy_rows().start()
-    pl.when(x == 1)(lambda: own(LAST))
     own(CPL)
     cross_own(False)
+    pl.when(x == 1)(lambda: own(LAST))
     for copy in loads:
         copy.wait()
     rr_give[...] = rrhs_ref[:, pl.ds(there, hcols)].T.astype(BF16)
     copy_rrhs().start()
     pl.when(x == 0)(lambda: own(LAST))
-    near(INV)
-    near(LAST)
+    near(INV, 1)
     alive = lax.broadcasted_iota(jnp.int32, (1, order), 1) < order_ref[0]
     src_t[...] = jnp.where(alive, rhs_ref[...].T, 0.0).astype(BF16)
-    near(CPL)
-    far(INV)
+    near(CPL, 1)
+    near(INV, 2)
+    far(LAST, 0)
+    far(INV, 0)
+    own(B2)
+    near(LAST, 1)
+    near(CPL, 2)
+    near(INV, *range(3, lines))
+    far(INV, 1)
+    far(CPL, 0)
+    own(B1)
+    near(B2, 1)
+    near(LAST, 2)
+    near(CPL, *range(3, lines))
+    far(INV, *range(2, lines))
+    far(CPL, 1)
+    own(B0)
     index = rows_ref[...]
     turn(0, index)
     scatter_ones(0)
-    own(B2)
-    far(LAST)
-    near(B2)
     over_core(INV)
+    near(B1, 1)
+    near(B2, 2)
+    near(LAST, *range(3, lines))
     for q in range(order // part):
         at = pl.ds(q * part, part)
         upto = pl.ds(0, (q + 1) * part)
         solved_t[:, at] = jnp.where(
             alive[:, q * part:(q + 1) * part], dot_t(src_t[:, upto], inv[at, upto]), 0.0
         )
-    own(B1)
-    own(B0)
-    far(CPL)
-    near(B1)
-    near(B0)
+    far(CPL, *range(2, lines))
+    near(B0, 1)
+    near(B1, 2)
+    near(B2, *range(3, lines))
     over_core(CPL)
     upd_t[...] = dot_t(solved_t[...].astype(BF16), cpl[...]).astype(BF16)
     copy_update().start()
-    far(B2)
-    crossed()
+    far(B2, 0, 1)
+    near(B0, 2)
+    near(B1, *range(3, lines))
     mine = pl.ds(pl.multiple_of(x * own_rows, own_rows), own_rows)
     theirs = pl.ds(pl.multiple_of((1 - x) * own_rows, own_rows), own_rows)
     copy_rrhs().wait_recv()
@@ -338,14 +350,16 @@
     for i in range(hott.shape[2] // block):
         at = pl.ds(i * block, block)
         base_t[:, at] = base_t[:, at] - dot_n(mine_upd, hott[0, :, at])
+    near(B0, *range(3, lines))
     copy_rows().wait_recv()
     turn(1, rows_peer[...])
     scatter_ones(1)
-    far(B1)
-    far(B0)
+    crossed()
+    far(B2, *range(2, lines))
+    over_core(LAST)
     gather_ones(index)
-    over_core(LAST)
     over_core(CROSS)
+    far(B1, 0, 1)
     copy_update().wait_recv()
     for i in range(hott.shape[2] // block):
         at = pl.ds(i * block, block)
@@ -354,6 +368,10 @@
     blocks = chunks // 2
     for b in reversed(range(blocks)):
         if b < blocks - 1:
+            if b == 1:
+                far(B1, *range(2, lines))
+            if b == 0:
+                far(B0, *range(lines))
             over_core((B0, B1, B2)[b])
         for k in (2 * b + 1, 2 * b):
             upto = pl.ds(0, (k + 1) * part)
@@ -443,8 +461,8 @@
     child_out, root_out = pl.pallas_call(
         functools.partial(kernel, lines),
         out_shape=(
-            jax.ShapeDtypeStruct((order, cols), F32),
-            jax.ShapeDtypeStruct((own_rows, cols), F32),
+            pltpu.VMEM((order, cols), F32),
+            pltpu.VMEM((own_rows, cols), F32),
         ),
         in_specs=[anywhere] * 2 + [vmem] * 3 + [smem, vmem],
         out_specs=(vmem, vmem),
@@ -471,7 +489,7 @@
             pltpu.VMEM((cols, root_order), BF16),
             pltpu.VMEM((half, order), BF16),
             dma((7, n)),
-            dma((6, 2, lines)),
+            dma((6, 2, 2, lines)),
             dma((6, lines)),
             dma((2, lines)),
             dma((7, 2, lines)),

time: 79.9 us -> 71.6 us (0.90)
  the two profiles are of different devices: /device:TPU:24 before, /device:TPU:0 now
where the time goes in v2:
time: 71.6 us; the launch traced here: 71.5 us
  Pallas kernels  68.3 us (95%)
  local copies, waits for them, and re-layouts  1.94 us (3%)
  between operations  1.29 us (2%)
    pallas_call x1, Pallas kernels, fused(): pl.pallas_call(functools.partial(kernel, lines), out_shape=(pltpu.VMEM((o...  68.3 us
    unnamed x2, local copies, waits for them, and re-layouts  1.94 us

profile of v2, /device:TPU:0, one launch (start us, length us, event | category | flops | bytes accessed | tf_op | source)
XLA Modules:
  0.0 71.5 jit_solution(18343579011608924847)
XLA Ops:
  1.3 68.3 %shard_map.86 = (f32[1024,256]{1,0:T(8,128)S(1)}, f32[1024,256]{1,0:T(8,128)S(1)}) custom-call(f32[1024,256]{1,0:T(8,128)} %bitcast.5, f32[1024,256]{1,0:T(8,128)} %rrhs_any.1, bf16[64,1024]{1,0:T(8,128)(2,1)} %bitcast.6, bf16[64,1024]{1,0:T(8,128)(2,1)} %bitcast.7, bf16[1024,128]{1,0:T(8,128)(2,1)} %rinv_ref.1, s32[1]{0:T(128)S(6)} %copy.13.order_ref, ...), custom_call_target="tpu_custom_call" | custom-call | tf_op jit(solution)/shard_map/pallas_call | solution.py:461
  69.5 1.0 %copy.11 = f32[1,1024,256]{2,1,0:T(8,128)} copy(f32[1,1024,256]{2,1,0:T(8,128)S(1)} %bitcast.4) | data formatting | bytes 2097152
  70.5 1.0 %copy.12 = f32[1024,256]{1,0:T(8,128)} copy(f32[1024,256]{1,0:T(8,128)S(1)} %get-tuple-element.7) | data formatting | bytes 2097152

commit v3 on v2

--- a/solution.py
+++ b/solution.py
@@ -22,8 +22,8 @@
 
 
 def kernel(
-    lines, rhs_any, rrhs_any, inv_ref, cpl_ref, rinv_ref, order_ref, rows_ref, child_out, root_out,
-    inv, cpl, root, hot, hott, column, rows_peer, rhs_ref, rrhs_ref,
+    lines, rhs_any, rrhs_any, inv_ref, cpl_ref, rinv_ref, order_ref, rows_any, child_out, root_out,
+    inv, cpl, root, hot, hott, column, rows_ref, rows_peer, rhs_ref, rrhs_ref,
     src_t, solved_t, upd_t, upd_peer, rr_give, rr_take, base_t, take, rr_t, sol_t, sol_b, res_t,
     recv, send_z, send_y, send_x, send_c, early_s, rows_r, rr_r, up_s, up_r, bk_s, bk_r, lay,
 ):
@@ -48,13 +48,6 @@
     def dev(zz, yy, cc, xx):
         return {"src": src_of(zz, yy, cc), "sub": xx}
 
-    loads = [
-        pltpu.make_async_copy(rhs_any, rhs_ref, lay.at[0]),
-        pltpu.make_async_copy(rrhs_any, rrhs_ref, lay.at[1]),
-    ]
-    for copy in loads:
-        copy.start()
-
     barrier = pltpu.get_barrier_semaphore()
 
     def hello(device):
@@ -68,6 +61,12 @@
         pl.when(zz != z)(lambda: hello(dev(zz, y, core, x)))
         return 0
     lax.fori_loop(0, lines, greet, 0)
+
+    loads = [
+        pltpu.make_async_copy(rhs_any, rhs_ref, lay.at[0]),
+        pltpu.make_async_copy(rrhs_any, rrhs_ref, lay.at[1]),
+        pltpu.make_async_copy(rows_any, rows_ref, lay.at[8]),
+    ]
 
     def strip_ref(which, s):
         r = pl.multiple_of(s * strip, strip)
@@ -88,7 +87,7 @@
         )
         for i in range(per)
     ]
-    for copy in placing:
+    for copy in placing + loads:
         copy.start()
 
     last = chunks - 2 + x
@@ -287,92 +286,51 @@
     for copy in placing:
         copy.wait()
 
-    own(INV)
-    early(False)
-    copy_rows().start()
-    own(CPL)
-    cross_own(False)
-    pl.when(x == 1)(lambda: own(LAST))
-    for copy in loads:
-        copy.wait()
-    rr_give[...] = rrhs_ref[:, pl.ds(there, hcols)].T.astype(BF16)
-    copy_rrhs().start()
-    pl.when(x == 0)(lambda: own(LAST))
-    near(INV, 1)
     alive = lax.broadcasted_iota(jnp.int32, (1, order), 1) < order_ref[0]
-    src_t[...] = jnp.where(alive, rhs_ref[...].T, 0.0).astype(BF16)
-    near(CPL, 1)
-    near(INV, 2)
-    far(LAST, 0)
-    far(INV, 0)
-    own(B2)
-    near(LAST, 1)
-    near(CPL, 2)
-    near(INV, *range(3, lines))
-    far(INV, 1)
-    far(CPL, 0)
-    own(B1)
-    near(B2, 1)
-    near(LAST, 2)
-    near(CPL, *range(3, lines))
-    far(INV, *range(2, lines))
-    far(CPL, 1)
-    own(B0)
-    index = rows_ref[...]
-    turn(0, index)
-    scatter_ones(0)
-    over_core(INV)
-    near(B1, 1)
-    near(B2, 2)
-    near(LAST, *range(3, lines))
-    for q in range(order // part):
+    mine = pl.ds(pl.multiple_of(x * own_rows, own_rows), own_rows)
+    theirs = pl.ds(pl.multiple_of((1 - x) * own_rows, own_rows), own_rows)
+    blocks = chunks // 2
+
+    def give_rhs():
+        loads[1].wait()
+        rr_give[...] = rrhs_ref[:, pl.ds(there, hcols)].T.astype(BF16)
+        base_t[:, mine] = rrhs_ref[:, pl.ds(here, hcols)].T
+        copy_rrhs().start()
+
+    def source():
+        loads[0].wait()
+        src_t[...] = jnp.where(alive, rhs_ref[...].T, 0.0).astype(BF16)
+
+    def ones(slot, index_ref):
+        turn(slot, index_ref[...])
+        scatter_ones(slot)
+
+    def solve(q):
         at = pl.ds(q * part, part)
         upto = pl.ds(0, (q + 1) * part)
         solved_t[:, at] = jnp.where(
             alive[:, q * part:(q + 1) * part], dot_t(src_t[:, upto], inv[at, upto]), 0.0
         )
-    far(CPL, *range(2, lines))
-    near(B0, 1)
-    near(B1, 2)
-    near(B2, *range(3, lines))
-    over_core(CPL)
-    upd_t[...] = dot_t(solved_t[...].astype(BF16), cpl[...]).astype(BF16)
-    copy_update().start()
-    far(B2, 0, 1)
-    near(B0, 2)
-    near(B1, *range(3, lines))
-    mine = pl.ds(pl.multiple_of(x * own_rows, own_rows), own_rows)
-    theirs = pl.ds(pl.multiple_of((1 - x) * own_rows, own_rows), own_rows)
-    copy_rrhs().wait_recv()
-    base_t[:, mine] = rrhs_ref[:, pl.ds(here, hcols)].T
-    base_t[:, theirs] = rr_take[...].astype(F32)
-    mine_upd = upd_t[pl.ds(here, hcols), :]
-    for i in range(hott.shape[2] // block):
-        at = pl.ds(i * block, block)
-        base_t[:, at] = base_t[:, at] - dot_n(mine_upd, hott[0, :, at])
-    near(B0, *range(3, lines))
-    copy_rows().wait_recv()
-    turn(1, rows_peer[...])
-    scatter_ones(1)
-    crossed()
-    far(B2, *range(2, lines))
-    over_core(LAST)
-    gather_ones(index)
-    over_core(CROSS)
-    far(B1, 0, 1)
-    copy_update().wait_recv()
-    for i in range(hott.shape[2] // block):
-        at = pl.ds(i * block, block)
-        take[:, at] = (base_t[:, at] - dot_n(upd_peer[...], hott[1, :, at])).astype(BF16)
-
-    blocks = chunks // 2
-    for b in reversed(range(blocks)):
-        if b < blocks - 1:
-            if b == 1:
-                far(B1, *range(2, lines))
-            if b == 0:
-                far(B0, *range(lines))
-            over_core((B0, B1, B2)[b])
+
+    def update():
+        upd_t[...] = dot_t(solved_t[...].astype(BF16), cpl[...]).astype(BF16)
+        copy_update().start()
+
+    def scatter_mine():
+        copy_rrhs().wait_recv()
+        base_t[:, theirs] = rr_take[...].astype(F32)
+        mine_upd = upd_t[pl.ds(here, hcols), :]
+        for i in range(hott.shape[2] // block):
+            at = pl.ds(i * block, block)
+            base_t[:, at] = base_t[:, at] - dot_n(mine_upd, hott[0, :, at])
+
+    def scatter_theirs():
+        copy_update().wait_recv()
+        for i in range(hott.shape[2] // block):
+            at = pl.ds(i * block, block)
+            take[:, at] = (base_t[:, at] - dot_n(upd_peer[...], hott[1, :, at])).astype(BF16)
+
+    def root_block(b):
         for k in (2 * b + 1, 2 * b):
             upto = pl.ds(0, (k + 1) * part)
             rr_t[:, pl.ds(k * part, part)] = dot_t(take[:, upto], root[k, :, upto]).astype(BF16)
@@ -388,13 +346,81 @@
         sol_t[:, at_high] = s_high
         sol_b[pl.ds(here, hcols), at_low] = s_low.astype(BF16)
         sol_b[pl.ds(here, hcols), at_high] = s_high.astype(BF16)
-        if b < blocks - 1:
-            back(b + 1).start()
         for a in reversed(range(b)):
             at = pl.ds(a * block, block)
             more = dot_n(r_low, root[low, :, at]) + dot_n(r_high, root[high, :, at])
             sol_t[:, at] = more if b == blocks - 1 else sol_t[:, at] + more
-    back(0).start()
+        back(b).start()
+
+    own(INV)
+    own(CPL)
+    loads[2].wait()
+    copy_rows().start()
+    early(False)
+    cross_own(False)
+    pl.when(x == 0)(lambda: own(LAST))
+    source()
+    copy_rows().wait_recv()
+    ones(1, rows_peer)
+    near(INV, 1)
+    pl.when(x == 1)(lambda: own(LAST))
+    near(CPL, 1)
+    near(INV, 2)
+    give_rhs()
+    own(B2)
+    near(INV, 3)
+    near(CPL, 2)
+    far(INV, 0)
+    far(LAST, 0)
+    far(INV, 3, 2)
+    near(CPL, 3)
+    far(INV, 1)
+    near(LAST, 1)
+    far(CPL, 0)
+    over_core(INV)
+    far(CPL, 1)
+    solve(0)
+    near(LAST, 2)
+    near(B2, 1)
+    far(CPL, 2)
+    own(B1)
+    solve(3)
+    solve(2)
+    far(CPL, 3)
+    near(LAST, 3)
+    own(B0)
+    over_core(CPL)
+    far(B2, 0)
+    solve(1)
+    near(B2, 2)
+    update()
+    near(B1, 1)
+    near(B2, 3)
+    crossed()
+    far(B2, 1)
+    ones(0, rows_ref)
+    scatter_mine()
+    near(B1, 2, 3)
+    far(B1, 0)
+    far(B0, 0)
+    over_core(LAST)
+    scatter_theirs()
+    far(B1, 2)
+    far(B2, 2, 3)
+    near(B0, 2, 1)
+    over_core(CROSS)
+    root_block(3)
+    far(B1, 3)
+    over_core(B2)
+    far(B1, 1)
+    root_block(2)
+    near(B0, 3)
+    over_core(B1)
+    gather_ones(rows_ref[...])
+    root_block(1)
+    far(B0, 1, 3, 2)
+    over_core(B0)
+    root_block(0)
 
     def finish(first, picked):
         rows = pl.ds(first, hcols)
@@ -409,6 +435,27 @@
 
     finish(here, dot_n(sol_b[pl.ds(here, hcols), :], hot[...]))
     root_out[:, pl.ds(here, hcols)] = sol_t[:, mine].T
+    early(True)
+    cross_own(True)
+    copy_rows().wait_send()
+    copy_rrhs().wait_send()
+    copy_update().wait_send()
+    for which in (INV, CPL, LAST, B2, B1, B0):
+        for away in (False, True):
+            def step(zz, _, which=which, away=away):
+                sends(which, zz, away, True)
+                return 0
+            lax.fori_loop(0, lines, step, 0)
+
+    def step(k, _):
+        s = src_of(k // 2, k % 2, core)
+
+        @pl.when(jnp.logical_or(s != me, x == 0))
+        def _():
+            push(CROSS, s, send_c.at[CROSS, k % 2, k // 2], dev(z, y, 1 - core, x), True)
+        return 0
+    lax.fori_loop(0, 2 * lines, step, 0)
+
     for a in range(1, blocks):
         back(a).wait_recv()
     upper = pl.ds(block, (blocks - 1) * block)
@@ -418,29 +465,8 @@
     picked += dot_n(sol_b[pl.ds(there, hcols), lower], hot[lower, :])
     finish(there, picked)
     root_out[:, pl.ds(there, hcols)] = sol_b[pl.ds(there, hcols), mine].astype(F32).T
-
-    early(True)
-    cross_own(True)
-    copy_rows().wait_send()
-    copy_rrhs().wait_send()
-    copy_update().wait_send()
     for a in range(blocks):
         back(a).wait_send()
-    for which in (INV, CPL, LAST, B2, B1, B0):
-        for away in (False, True):
-            def step(zz, _, which=which, away=away):
-                sends(which, zz, away, True)
-                return 0
-            lax.fori_loop(0, lines, step, 0)
-
-    def step(k, _):
-        s = src_of(k // 2, k % 2, core)
-
-        @pl.when(jnp.logical_or(s != me, x == 0))
-        def _():
-            push(CROSS, s, send_c.at[CROSS, k % 2, k // 2], dev(z, y, 1 - core, x), True)
-        return 0
-    lax.fori_loop(0, 2 * lines, step, 0)
 
 
 def fused(child_rhs, root_rhs, child_inverse, coupling_block, root_inverse, child_orders, coupling_rows):
@@ -464,7 +490,7 @@
             pltpu.VMEM((order, cols), F32),
             pltpu.VMEM((own_rows, cols), F32),
         ),
-        in_specs=[anywhere] * 2 + [vmem] * 3 + [smem, vmem],
+        in_specs=[anywhere] * 5 + [smem, anywhere],
         out_specs=(vmem, vmem),
         scratch_shapes=[
             pltpu.VMEM((order, order), BF16),
@@ -473,6 +499,7 @@
             pltpu.VMEM((root_order, couples), BF16),
             pltpu.VMEM((2, couples, root_order), BF16),
             pltpu.VMEM((2, couples, width), jnp.int32),
+            pltpu.VMEM((1, couples), jnp.int32),
             pltpu.VMEM((1, couples), jnp.int32),
             pltpu.VMEM((order, cols), F32),
             pltpu.VMEM((own_rows, cols), F32),
@@ -500,7 +527,7 @@
             dma,
             dma((4,)),
             dma((4,)),
-            dma((8,)),
+            dma((9,)),
         ],
         compiler_params=pltpu.CompilerParams(
             collective_id=0, has_side_effects=True, vmem_limit_bytes=60 * 1024 * 1024

time: 71.6 us -> 64.2 us (0.90)
  Pallas kernels: 68.3 us -> 60.5 us
    pallas_call x1, Pallas kernels: 68.3 us -> 60.5 us  [fused(): pl.pallas_call(functools.partial(kernel, lines), out_shape=(pltpu.VMEM((o...]
where the time goes in v3:
time: 64.2 us; the launch traced here: 63.7 us
  Pallas kernels  60.5 us (94%)
  local copies, waits for them, and re-layouts  1.94 us (3%)
  between operations  1.29 us (2%)
    pallas_call x1, Pallas kernels, fused(): pl.pallas_call(functools.partial(kernel, lines), out_shape=(pltpu.VMEM((o...  60.5 us
    unnamed x2, local copies, waits for them, and re-layouts  1.94 us

profile of v3, /device:TPU:0, one launch (start us, length us, event | category | flops | bytes accessed | tf_op | source)
XLA Modules:
  0.0 63.7 jit_solution(7468329958978890555)
XLA Ops:
  1.3 60.5 %shard_map.86 = (f32[1024,256]{1,0:T(8,128)S(1)}, f32[1024,256]{1,0:T(8,128)S(1)}) custom-call(f32[1024,256]{1,0:T(8,128)} %bitcast.5, f32[1024,256]{1,0:T(8,128)} %rrhs_any.1, bf16[64,1024]{1,0:T(8,128)(2,1)} %bitcast.6, bf16[64,1024]{1,0:T(8,128)(2,1)} %bitcast.7, bf16[1024,128]{1,0:T(8,128)(2,1)} %rinv_ref.1, s32[1]{0:T(128)S(6)} %copy.13.order_ref, ...), custom_call_target="tpu_custom_call" | custom-call | tf_op jit(solution)/shard_map/pallas_call | solution.py:487
  61.8 1.0 %copy.11 = f32[1,1024,256]{2,1,0:T(8,128)} copy(f32[1,1024,256]{2,1,0:T(8,128)S(1)} %bitcast.4) | data formatting | bytes 2097152
  62.8 1.0 %copy.12 = f32[1024,256]{1,0:T(8,128)} copy(f32[1024,256]{1,0:T(8,128)S(1)} %get-tuple-element.7) | data formatting | bytes 2097152

commit v4 on v3

--- a/solution.py
+++ b/solution.py
@@ -57,10 +57,13 @@
     hello(dev(z, y, 1 - core, x))
     hello(dev(z, y, core, 1 - x))
 
-    def greet(zz, _):
-        pl.when(zz != z)(lambda: hello(dev(zz, y, core, x)))
-        return 0
-    lax.fori_loop(0, lines, greet, 0)
+    @pl.when(z > 0)
+    def _():
+        hello(dev(z - 1, y, core, x))
+
+    @pl.when(z < lines - 1)
+    def _():
+        hello(dev(z + 1, y, core, x))
 
     loads = [
         pltpu.make_async_copy(rhs_any, rhs_ref, lay.at[0]),
@@ -282,7 +285,9 @@
             at = lax.broadcasted_iota(jnp.int32, (part, order), 0) + r
             hot[pl.ds(r, part), :] = jnp.where(at == index, 1.0, 0.0).astype(BF16)
 
-    pl.semaphore_wait(barrier, lines + 2)
+    inner = jnp.logical_and(z > 0, z < lines - 1)
+    pl.when(inner)(lambda: pl.semaphore_wait(barrier, 5))
+    pl.when(jnp.logical_not(inner))(lambda: pl.semaphore_wait(barrier, 4))
     for copy in placing:
         copy.wait()
 

time: 64.2 us -> 63.5 us (0.989)
  no operation moved by 1% of the time
where the time goes in v4:
time: 63.5 us; the launch traced here: 63.2 us
  Pallas kernels  60 us (94%)
  local copies, waits for them, and re-layouts  1.94 us (3%)
  between operations  1.29 us (2%)
    pallas_call x1, Pallas kernels, fused(): pl.pallas_call(functools.partial(kernel, lines), out_shape=(pltpu.VMEM((o...  60 us
    unnamed x2, local copies, waits for them, and re-layouts  1.94 us

profile of v4, /device:TPU:0, one launch (start us, length us, event | category | flops | bytes accessed | tf_op | source)
XLA Modules:
  0.0 63.2 jit_solution(11398221839499780858)
XLA Ops:
  1.3 60.0 %shard_map.86 = (f32[1024,256]{1,0:T(8,128)S(1)}, f32[1024,256]{1,0:T(8,128)S(1)}) custom-call(f32[1024,256]{1,0:T(8,128)} %bitcast.5, f32[1024,256]{1,0:T(8,128)} %rrhs_any.1, bf16[64,1024]{1,0:T(8,128)(2,1)} %bitcast.6, bf16[64,1024]{1,0:T(8,128)(2,1)} %bitcast.7, bf16[1024,128]{1,0:T(8,128)(2,1)} %rinv_ref.1, s32[1]{0:T(128)S(6)} %copy.13.order_ref, ...), custom_call_target="tpu_custom_call" | custom-call | tf_op jit(solution)/shard_map/pallas_call | solution.py:492
  61.3 1.0 %copy.11 = f32[1,1024,256]{2,1,0:T(8,128)} copy(f32[1,1024,256]{2,1,0:T(8,128)S(1)} %bitcast.4) | data formatting | bytes 2097152
  62.2 1.0 %copy.12 = f32[1024,256]{1,0:T(8,128)} copy(f32[1024,256]{1,0:T(8,128)S(1)} %get-tuple-element.7) | data formatting | bytes 2097152

commit v5 on v4

--- a/solution.py
+++ b/solution.py
@@ -288,8 +288,7 @@
     inner = jnp.logical_and(z > 0, z < lines - 1)
     pl.when(inner)(lambda: pl.semaphore_wait(barrier, 5))
     pl.when(jnp.logical_not(inner))(lambda: pl.semaphore_wait(barrier, 4))
-    for copy in placing:
-        copy.wait()
+    placing[0].wait()
 
     alive = lax.broadcasted_iota(jnp.int32, (1, order), 1) < order_ref[0]
     mine = pl.ds(pl.multiple_of(x * own_rows, own_rows), own_rows)
@@ -358,7 +357,10 @@
         back(b).start()
 
     own(INV)
+    placing[1].wait()
     own(CPL)
+    for copy in placing[2:]:
+        copy.wait()
     loads[2].wait()
     copy_rows().start()
     early(False)
@@ -421,11 +423,12 @@
     root_block(2)
     near(B0, 3)
     over_core(B1)
-    gather_ones(rows_ref[...])
     root_block(1)
     far(B0, 1, 3, 2)
     over_core(B0)
     root_block(0)
+
+    gather_ones(rows_ref[...])
 
     def finish(first, picked):
         rows = pl.ds(first, hcols)

time: 63.5 us -> 63.4 us (level)
  no operation moved by 1% of the time
where the time goes in v5:
time: 63.4 us; the launch traced here: 63.2 us
  Pallas kernels  60 us (95%)
  local copies, waits for them, and re-layouts  1.94 us (3%)
  between operations  1.29 us (2%)
    pallas_call x1, Pallas kernels, fused(): pl.pallas_call(functools.partial(kernel, lines), out_shape=(pltpu.VMEM((o...  60 us
    unnamed x2, local copies, waits for them, and re-layouts  1.94 us

profile of v5, /device:TPU:0, one launch (start us, length us, event | category | flops | bytes accessed | tf_op | source)
XLA Modules:
  0.0 63.2 jit_solution(1830718427191011810)
XLA Ops:
  1.3 60.0 %shard_map.86 = (f32[1024,256]{1,0:T(8,128)S(1)}, f32[1024,256]{1,0:T(8,128)S(1)}) custom-call(f32[1024,256]{1,0:T(8,128)} %bitcast.5, f32[1024,256]{1,0:T(8,128)} %rrhs_any.1, bf16[64,1024]{1,0:T(8,128)(2,1)} %bitcast.6, bf16[64,1024]{1,0:T(8,128)(2,1)} %bitcast.7, bf16[1024,128]{1,0:T(8,128)(2,1)} %rinv_ref.1, s32[1]{0:T(128)S(6)} %copy.13.order_ref, ...), custom_call_target="tpu_custom_call" | custom-call | tf_op jit(solution)/shard_map/pallas_call | solution.py:495
  61.3 1.0 %copy.11 = f32[1,1024,256]{2,1,0:T(8,128)} copy(f32[1,1024,256]{2,1,0:T(8,128)S(1)} %bitcast.4) | data formatting | bytes 2097152
  62.2 1.0 %copy.12 = f32[1024,256]{1,0:T(8,128)} copy(f32[1024,256]{1,0:T(8,128)S(1)} %get-tuple-element.7) | data formatting | bytes 2097152
